TPU v7x, 32 devices: a whole 2x2x4 slice. The times are simulated.
32 devices in a mesh: dp: 8 (over z, x), expert: 4 (over y, core).
Axes of the slice: x: 2, y: 2, z: 4, core: 2. Of those that a mesh axis runs over, the one named last changes fastest.
Arguments:
- tokens: bfloat16 [4096, 1024], P(('dp', 'expert')), may hold values from -24 to 24
- cotangent: bfloat16 [4096, 1024], P(('dp', 'expert')), may hold values from -6 to 6
- prefix: int32 [8], P('dp'), may hold values from 51 to 256
- expert_choice: int32 [4096, 1], P(('dp', 'expert')), may hold values from 0 to 3; in each aligned block of 128 rows (0 to 127, 128 to 255, ...) at most 64 rows name the same one
- norm1_gain: bfloat16 [1024], P(('dp', 'expert')), may hold values from 0.099609375 to 1.8984375
- w_qkv: bfloat16 [1024, 3072], P(('dp', 'expert')), may hold values from -0.1875 to 0.1875
- w_out: bfloat16 [1024, 1024], P(('dp', 'expert')), may hold values from -1.5 to 1.5
- norm2_gain: bfloat16 [1024], P(('dp', 'expert')), may hold values from 0.099609375 to 1.8984375
- w_up: bfloat16 [1024, 4096], P(('dp', 'expert')), may hold values from -0.1875 to 0.1875
- w_down: bfloat16 [4096, 1024], P(('dp', 'expert')), may hold values from -0.09375 to 0.09375
- w_router: bfloat16 [1024, 4], P(('dp', 'expert')), may hold values from -0.125 to 0.125
- w_mix: bfloat16 [1024, 2], P(('dp', 'expert')), may hold values from -0.1875 to 0.1875
- expert_up: bfloat16 [4096, 4, 1024], P('dp', 'expert'), may hold values from -0.1875 to 0.1875
- expert_down: bfloat16 [4096, 4, 1024], P('dp', 'expert'), may hold values from -0.375 to 0.375
Outputs:
- output: float32 [4096, 1024], P(('dp', 'expert'))
- grad_tokens: float32 [4096, 1024], P(('dp', 'expert'))
- grad_norm1_gain: float32 [1024], P(('dp', 'expert'))
- grad_w_qkv: float32 [1024, 3072], P(('dp', 'expert'))
- grad_w_out: float32 [1024, 1024], P(('dp', 'expert'))
- grad_norm2_gain: float32 [1024], P(('dp', 'expert'))
- grad_w_up: float32 [1024, 4096], P(('dp', 'expert'))
- grad_w_down: float32 [4096, 1024], P(('dp', 'expert'))
- grad_w_router: float32 [1024, 4], P(('dp', 'expert'))
- grad_w_mix: float32 [1024, 2], P(('dp', 'expert'))
- grad_expert_up: float32 [4096, 4, 1024], P('dp', 'expert')
- grad_expert_down: float32 [4096, 4, 1024], P('dp', 'expert')
- rms_mid: float32 [], replicated
- rms_attn: float32 [], replicated
- rms_ffn: float32 [], replicated
- rms_out: float32 [], replicated
Inputs may be any that keep to these rules, and one draw needn't show every extreme that they name: `expert_choice`: among the 128 rows of one device no expert is chosen more than 64 times.
All inputs are finite; a program needn't handle non-finite values.
Results may differ from a plain program's by a relative error of at most 0.033.
Values may be sent and summed in bfloat16 or wider, within the bound.
A program may use at most 192 MiB of HBM per device.

v0:
```python
import jax
import jax.numpy as jnp
from jax import lax
from jax.sharding import PartitionSpec as P

HEAD = 64
EPS = 1e-05
NEG_FILL = -1e30
HIGHEST = lax.Precision.HIGHEST
ROWS_AXIS = (((0,), (0,)), ((), ()))
COLS_AXIS = (((1,), (1,)), ((), ()))


def layer_norm(values, norm_gain):
    row_mean = jnp.mean(values, axis=-1, keepdims=True)
    centered = values - row_mean
    inverse = lax.rsqrt(jnp.mean(centered * centered, axis=-1, keepdims=True) + EPS)
    normed = centered * inverse
    return (normed * norm_gain, normed, inverse)


def norm_back(grad_out, normed, inverse, norm_gain):
    scaled = grad_out * norm_gain
    mean_one = jnp.mean(scaled, axis=-1, keepdims=True)
    mean_two = jnp.mean(scaled * normed, axis=-1, keepdims=True)
    return (inverse * (scaled - mean_one - normed * mean_two), jnp.sum(grad_out * normed, axis=0))


def gelu_tanh(values):
    return jax.nn.gelu(values, approximate=True)


def gelu_back(pre_act, grad_act):
    return jax.vjp(gelu_tanh, pre_act)[1](grad_act)[0]


def softmax_rows(logits):
    shifted = logits - jnp.max(logits, axis=-1, keepdims=True)
    weights = jnp.exp(shifted)
    return weights / jnp.sum(weights, axis=-1, keepdims=True)


def contract_rows(left_side, right_side):
    return lax.dot_general(left_side, right_side, ROWS_AXIS, preferred_element_type=jnp.float32)


def contract_cols(left_side, right_side):
    return lax.dot_general(left_side, right_side, COLS_AXIS, preferred_element_type=jnp.float32)


def precise_rows(left_side, right_side):
    return lax.dot_general(
        left_side, right_side, ROWS_AXIS, precision=HIGHEST, preferred_element_type=jnp.float32
    )


def precise_cols(left_side, right_side):
    return lax.dot_general(
        left_side, right_side, COLS_AXIS, precision=HIGHEST, preferred_element_type=jnp.float32
    )


def per_device(
    tokens,
    cotangent,
    prefix,
    expert_choice,
    norm1_gain,
    w_qkv,
    w_out,
    norm2_gain,
    w_up,
    w_down,
    w_router,
    w_mix,
    expert_up,
    expert_down,
):
    local_rows, model_width = tokens.shape
    experts = lax.axis_size("expert")
    replicas = lax.axis_size("dp")
    capacity = 2 * local_rows // experts
    cut_width = model_width // experts
    head_count = cut_width // HEAD
    ff_cut = w_up.shape[1] // experts
    row_share = w_qkv.shape[0]
    ff_share = w_down.shape[0]
    stride = replicas // experts
    my_block = lax.axis_index("dp") * experts + lax.axis_index("expert")
    score_scale = HEAD ** (-0.5)
    ff_own = replicas * ff_share

    def spread(rows_low):
        return lax.all_gather(rows_low, "expert", axis=0, tiled=True)

    def fold(partial_sums):
        return lax.psum_scatter(
            partial_sums.astype(jnp.bfloat16), "expert", scatter_dimension=0, tiled=True
        ).astype(jnp.float32)

    def swap(blocks):
        return lax.all_to_all(blocks, "expert", split_axis=0, concat_axis=0, tiled=True)

    def gather_dp(rows):
        return lax.all_gather(rows, "dp", axis=0, tiled=True)

    def scatter_dp(rows):
        return lax.psum_scatter(rows.astype(jnp.bfloat16), "dp", scatter_dimension=0, tiled=True)

    small = lax.all_gather(
        jnp.concatenate([norm1_gain[:, None], norm2_gain[:, None], w_router, w_mix], axis=1),
        ("dp", "expert"),
        axis=0,
        tiled=True,
    )
    gain_one = small[:, 0].astype(jnp.float32)
    gain_two = small[:, 1].astype(jnp.float32)
    router_w = small[:, 2 : 2 + experts]
    mix_w = small[:, 2 + experts :]
    qkv_out = jnp.moveaxis(w_qkv.reshape(row_share, 3, experts, cut_width), 2, 0)
    qkv_w = gather_dp(swap(qkv_out).reshape(experts * row_share, 3 * cut_width))
    out_rows = gather_dp(w_out)
    out_in = swap(out_rows.reshape(experts, stride * row_share, model_width))
    out_w = jnp.transpose(
        out_in.reshape(experts, stride, row_share, model_width), (1, 0, 2, 3)
    ).reshape(cut_width, model_width)
    up_out = jnp.moveaxis(w_up.reshape(row_share, replicas, experts, ff_share), 2, 0)
    up_w = gather_dp(swap(up_out).reshape(experts * row_share, ff_own))
    down_w = gather_dp(w_down)
    expert_in_w = expert_up[:, 0, :]
    expert_out_w = expert_down[:, 0, :]
    inputs = tokens.astype(jnp.float32)
    scaled_one, normed_one, inverse_one = layer_norm(inputs, gain_one)
    normed_all = spread(scaled_one.astype(jnp.bfloat16))
    seq_len = normed_all.shape[0]
    qkv_cut = jnp.dot(normed_all, qkv_w, preferred_element_type=jnp.float32).astype(jnp.bfloat16)
    queries = qkv_cut[:, :cut_width].reshape(seq_len, head_count, HEAD)
    keys = qkv_cut[:, cut_width : 2 * cut_width].reshape(seq_len, head_count, HEAD)
    values = qkv_cut[:, 2 * cut_width :].reshape(seq_len, head_count, HEAD)
    position = jnp.arange(seq_len, dtype=jnp.int32)
    visible = (position[None, :] <= position[:, None]) | (position[None, :] < prefix[0])
    masked = jnp.where(
        visible[None],
        jnp.einsum("qhd,khd->hqk", queries, keys, preferred_element_type=jnp.float32) * score_scale,
        NEG_FILL,
    )
    row_max = jnp.max(masked, axis=-1, keepdims=True)
    expd = jnp.exp(masked - row_max)
    probs = expd / jnp.sum(expd, axis=-1, keepdims=True)
    probs_low = probs.astype(jnp.bfloat16)
    attended_cut = (
        jnp.einsum("hqk,khd->qhd", probs_low, values, preferred_element_type=jnp.float32)
        .reshape(seq_len, cut_width)
        .astype(jnp.bfloat16)
    )
    attn_out = fold(jnp.dot(attended_cut, out_w, preferred_element_type=jnp.float32))
    middle = inputs + attn_out
    scaled_two, normed_two, inverse_two = layer_norm(middle, gain_two)
    hidden_low = scaled_two.astype(jnp.bfloat16)
    router_probs = softmax_rows(jnp.dot(hidden_low, router_w, preferred_element_type=jnp.float32))
    chosen = expert_choice[:, 0]
    onehot_int = (jnp.arange(experts, dtype=jnp.int32)[None, :] == chosen[:, None]).astype(
        jnp.int32
    )
    onehot = onehot_int.astype(jnp.float32)
    gate_prob = jnp.sum(router_probs * onehot, axis=-1)
    mix_coef = softmax_rows(jnp.dot(hidden_low, mix_w, preferred_element_type=jnp.float32))
    coef_dense = mix_coef[:, 0:1]
    coef_expert = (mix_coef[:, 1] * gate_prob)[:, None]
    grad_out = cotangent.astype(jnp.float32)
    grad_dense = (grad_out * coef_dense).astype(jnp.bfloat16)
    grad_expert = (grad_out * coef_expert).astype(jnp.bfloat16)
    row_id = jnp.arange(local_rows, dtype=jnp.int32)
    before = (row_id[:, None] > row_id[None, :]).astype(jnp.bfloat16)
    earlier = jnp.dot(before, onehot.astype(jnp.bfloat16), preferred_element_type=jnp.float32)
    slot_rank = jnp.sum(earlier * onehot, axis=-1).astype(jnp.int32)
    slot_index = chosen * capacity + slot_rank
    slot_rows = experts * capacity
    picks = (slot_index[:, None] == jnp.arange(slot_rows, dtype=jnp.int32)[None, :]).astype(
        jnp.bfloat16
    )
    send_rows = contract_rows(picks, jnp.concatenate([hidden_low, grad_expert], axis=1)).astype(
        jnp.bfloat16
    )
    received = swap(send_rows.reshape(experts, capacity, 2 * model_width))
    routed = gather_dp(received.reshape(slot_rows, 2 * model_width))
    routed_in = routed[:, :model_width]
    routed_grad = routed[:, model_width:]
    dense_rows = spread(jnp.concatenate([hidden_low, grad_dense], axis=1))
    hidden_all = dense_rows[:, :model_width]
    grad_dense_all = dense_rows[:, model_width:]
    dense_pre = jnp.dot(hidden_all, up_w, preferred_element_type=jnp.float32)
    dense_act = gelu_tanh(dense_pre).astype(jnp.bfloat16)
    grad_act_d = contract_cols(grad_dense_all, down_w)
    grad_pre_d = gelu_back(dense_pre, grad_act_d).astype(jnp.bfloat16)
    dense_sums = jnp.concatenate(
        [
            jnp.dot(dense_act, down_w, preferred_element_type=jnp.float32).astype(jnp.bfloat16),
            contract_cols(grad_pre_d, up_w).astype(jnp.bfloat16),
        ],
        axis=1,
    )
    dense_back = fold(dense_sums)
    dense_out = dense_back[:, :model_width]
    grad_w_down_cut = contract_rows(dense_act, grad_dense_all)
    grad_w_up_cut = contract_rows(hidden_all, grad_pre_d)
    pre_act = contract_cols(routed_in, expert_in_w)
    act_low = gelu_tanh(pre_act).astype(jnp.bfloat16)
    grad_act_e = contract_cols(routed_grad, expert_out_w)
    grad_pre_e = gelu_back(pre_act, grad_act_e).astype(jnp.bfloat16)
    expert_sums = jnp.concatenate(
        [
            jnp.dot(act_low, expert_out_w, preferred_element_type=jnp.float32).astype(jnp.bfloat16),
            jnp.dot(grad_pre_e, expert_in_w, preferred_element_type=jnp.float32).astype(
                jnp.bfloat16
            ),
        ],
        axis=1,
    )
    grad_expert_up = contract_rows(grad_pre_e, routed_in)
    grad_expert_down = contract_rows(act_low, routed_grad)
    expert_back = swap(scatter_dp(expert_sums).reshape(experts, capacity, 2 * model_width))
    expert_rows_all = jnp.dot(
        picks, expert_back.reshape(slot_rows, 2 * model_width), preferred_element_type=jnp.float32
    )
    expert_rows = expert_rows_all[:, :model_width]
    ffn_out = coef_dense * dense_out + coef_expert * expert_rows
    result = middle + ffn_out
    square_stats = jnp.stack(
        [
            jnp.sum(middle * middle),
            jnp.sum(attn_out * attn_out),
            jnp.sum(ffn_out * ffn_out),
            jnp.sum(result * result),
        ]
    )
    dense_dot = jnp.sum(grad_out * dense_out, axis=-1)
    expert_dot = jnp.sum(grad_out * expert_rows, axis=-1)
    coef_grad = jnp.stack([dense_dot, expert_dot * gate_prob], axis=-1)
    grad_mix = mix_coef * (coef_grad - jnp.sum(mix_coef * coef_grad, axis=-1, keepdims=True))
    gate_grad = expert_dot * mix_coef[:, 1]
    grad_router = (gate_grad * gate_prob)[:, None] * (onehot - router_probs)
    hidden_wide = hidden_low.astype(jnp.float32)
    grad_hidden = dense_back[:, model_width:] + expert_rows_all[:, model_width:]
    grad_hidden = (
        grad_hidden
        + precise_cols(grad_router, router_w.astype(jnp.float32))
        + precise_cols(grad_mix, mix_w.astype(jnp.float32))
    )
    grad_w_router = precise_rows(grad_router, hidden_wide)
    grad_w_mix = precise_rows(grad_mix, hidden_wide)
    grad_mid_norm, grad_gain_two = norm_back(grad_hidden, normed_two, inverse_two, gain_two)
    grad_middle = grad_out + grad_mid_norm
    grad_attn_all = spread(grad_middle.astype(jnp.bfloat16))
    grad_w_out_cut = contract_rows(attended_cut, grad_attn_all)
    grad_att_cut = (
        contract_cols(grad_attn_all, out_w).astype(jnp.bfloat16).reshape(seq_len, head_count, HEAD)
    )
    grad_probs = jnp.einsum(
        "qhd,khd->hqk", grad_att_cut, values, preferred_element_type=jnp.float32
    )
    row_delta = jnp.sum(probs * grad_probs, axis=-1, keepdims=True)
    grad_scores = (probs * (grad_probs - row_delta)).astype(jnp.bfloat16)
    grad_query = (
        jnp.einsum("hqk,khd->qhd", grad_scores, keys, preferred_element_type=jnp.float32)
        * score_scale
    )
    grad_key = (
        jnp.einsum("hqk,qhd->khd", grad_scores, queries, preferred_element_type=jnp.float32)
        * score_scale
    )
    grad_value = jnp.einsum(
        "hqk,qhd->khd", probs_low, grad_att_cut, preferred_element_type=jnp.float32
    )
    grad_qkv_cut = jnp.concatenate(
        [
            grad_query.reshape(seq_len, cut_width),
            grad_key.reshape(seq_len, cut_width),
            grad_value.reshape(seq_len, cut_width),
        ],
        axis=1,
    ).astype(jnp.bfloat16)
    grad_w_qkv_cut = contract_rows(normed_all, grad_qkv_cut)
    grad_normed = fold(contract_cols(grad_qkv_cut, qkv_w))
    grad_in_norm, grad_gain_one = norm_back(grad_normed, normed_one, inverse_one, gain_one)
    grad_tokens = grad_middle + grad_in_norm
    up_sum = swap(scatter_dp(grad_w_up_cut).reshape(experts, row_share, replicas, ff_share))
    grad_w_up = (
        jnp.transpose(up_sum, (1, 2, 0, 3)).reshape(row_share, experts * ff_own).astype(jnp.float32)
    )
    grad_w_down = scatter_dp(grad_w_down_cut).astype(jnp.float32)
    out_send = jnp.transpose(
        grad_w_out_cut.astype(jnp.bfloat16).reshape(stride, experts, row_share, model_width),
        (1, 0, 2, 3),
    )
    grad_w_out = scatter_dp(swap(out_send).reshape(replicas * row_share, model_width)).astype(
        jnp.float32
    )
    qkv_sum = swap(scatter_dp(grad_w_qkv_cut).reshape(experts, row_share, 3, cut_width))
    grad_w_qkv = (
        jnp.transpose(qkv_sum, (1, 2, 0, 3)).reshape(row_share, 3 * model_width).astype(jnp.float32)
    )
    totals = lax.psum(
        (
            jnp.concatenate(
                [grad_gain_one[None], grad_gain_two[None], grad_w_router, grad_w_mix], axis=0
            ),
            square_stats,
        ),
        ("dp", "expert"),
    )
    own = lax.dynamic_slice_in_dim(totals[0], my_block * row_share, row_share, 1)
    entry_count = local_rows * model_width * replicas * experts
    rms_values = jnp.sqrt(totals[1] / entry_count + 1e-06)
    return (
        result,
        grad_tokens,
        own[0],
        grad_w_qkv,
        grad_w_out,
        own[1],
        grad_w_up,
        grad_w_down,
        jnp.transpose(own[2 : 2 + experts]),
        jnp.transpose(own[2 + experts :]),
        grad_expert_up[:, None, :],
        grad_expert_down[:, None, :],
        rms_values[0],
        rms_values[1],
        rms_values[2],
        rms_values[3],
    )


def solution(mesh):
    return jax.shard_map(
        per_device,
        mesh=mesh,
        in_specs=(
            P(("dp", "expert"), None),
            P(("dp", "expert"), None),
            P("dp"),
            P(("dp", "expert"), None),
            P(("dp", "expert")),
            P(("dp", "expert"), None),
            P(("dp", "expert"), None),
            P(("dp", "expert")),
            P(("dp", "expert"), None),
            P(("dp", "expert"), None),
            P(("dp", "expert"), None),
            P(("dp", "expert"), None),
            P("dp", "expert", None),
            P("dp", "expert", None),
        ),
        out_specs=(
            P(("dp", "expert"), None),
            P(("dp", "expert"), None),
            P(("dp", "expert")),
            P(("dp", "expert"), None),
            P(("dp", "expert"), None),
            P(("dp", "expert")),
            P(("dp", "expert"), None),
            P(("dp", "expert"), None),
            P(("dp", "expert"), None),
            P(("dp", "expert"), None),
            P("dp", "expert", None),
            P("dp", "expert", None),
            P(),
            P(),
            P(),
            P(),
        ),
        check_vma=False,
    )
```

profile of v0, /device:TPU:0, one launch (start us, length us, event | category | flops | bytes accessed | tf_op | source)
XLA Modules:
  0.0 951.4 jit_solution(9734725191694061075)
XLA Ops:
  10.3 43.4 %all-gather = bf16[32,32,8]{1,2,0:T(8,128)(2,1)S(1)} all-gather(bf16[1,32,8]{1,2,0:T(8,128)(2,1)S(1)} %maximum_bitcast_fusion), channel_id=1, replica_groups=mesh['dp'=8,'expert'=4] {'dp','expert'}, dimensions={0}, use_global_device_ids=true | all-gather | bytes 16896 | tf_op jit(solution)/shard_map/all_gather | solution.py:110
  56.9 10.1 %all_to_all.40 = bf16[4,32,3,256]{3,1,2,0:T(8,128)(2,1)S(1)} all-to-all(bf16[4,32,3,256]{3,1,2,0:T(8,128)(2,1)S(1)} %copy.96), channel_id=1, replica_groups=mesh['dp'=8,'expert'=4] {'expert'}, dimensions={0} | all-to-all | bytes 393216 | tf_op jit(solution)/shard_map/all_to_all | solution.py:102
  67.9 33.8 %all_gather.30 = bf16[256,1024]{1,0:T(8,128)(2,1)} all-gather(bf16[32,1024]{1,0:T(8,128)(2,1)S(1)} %copy-done.26), channel_id=1, replica_groups=mesh['dp'=8,'expert'=4] {'dp'}, dimensions={0}, use_global_device_ids=true | all-gather | bytes 589824 | tf_op jit(solution)/shard_map/all_gather | solution.py:105
  106.0 7.9 all-to-all-done.1
  128.3 23.1 %reduce-scatter.9.cloned.1.call-done = bf16[128,1024]{1,0:T(8,128)(2,1)} async-done(((bf16[512,1024]{1,0:T(8,128)(2,1)}), bf16[128,1024]{1,0:T(8,128)(2,1)}) %reduce-scatter.9.cloned.1.call-update) | async-done | bytes 262160 | tf_op jit(solution)/shard_map/reduce_scatter | solution.py:97
  156.1 17.6 %all_to_all.41 = bf16[4,64,2048]{2,1,0:T(8,128)(2,1)} all-to-all(bf16[4,64,2048]{2,1,0:T(8,128)(2,1)S(1)} %bitcast.155), channel_id=1, replica_groups=mesh['dp'=8,'expert'=4] {'expert'}, dimensions={0} | all-to-all | bytes 2097152 | tf_op jit(solution)/shard_map/all_to_all | solution.py:102
  174.0 8.4 all_to_all.42
  185.3 113.0 %all-gather.19.cloned.1.call-done = bf16[2048,2048]{1,0:T(8,128)(2,1)} async-done(((bf16[256,2048]{1,0:T(8,128)(2,1)}), bf16[2048,2048]{1,0:T(8,128)(2,1)}) %all-gather.19.cloned.1.call-update) | async-done | bytes 8388624 | tf_op jit(solution)/shard_map/all_gather | solution.py:105
  298.3 4.8 fusion.14
  303.1 5.0 fusion.7
  316.8 8.4 pad_maximum_fusion
  325.4 22.7 %all-gather.15.cloned.1.call-done = bf16[1024,1024]{1,0:T(8,128)(2,1)} async-done(((bf16[128,1024]{1,0:T(8,128)(2,1)}), bf16[1024,1024]{1,0:T(8,128)(2,1)}) %all-gather.15.cloned.1.call-update) | async-done | bytes 2097168 | tf_op jit(solution)/shard_map/all_gather | solution.py:105
  348.2 23.1 %all-gather.13.cloned.1.call-done = bf16[512,2048]{1,0:T(8,128)(2,1)} async-done(((bf16[128,2048]{1,0:T(8,128)(2,1)}), bf16[512,2048]{1,0:T(8,128)(2,1)}) %all-gather.13.cloned.1.call-update) | async-done | bytes 2097168 | tf_op jit(solution)/shard_map/all_gather | solution.py:94
  375.9 46.6 %all-gather.17.cloned.1.call-done = bf16[1024,1024]{1,0:T(8,128)(2,1)} async-done(((bf16[128,1024]{1,0:T(8,128)(2,1)}), bf16[1024,1024]{1,0:T(8,128)(2,1)}) %all-gather.17.cloned.1.call-update) | async-done | bytes 2097168 | tf_op jit(solution)/shard_map/all_gather | solution.py:105
  432.8 139.7 %reduce-scatter.13.cloned.1.call-done = bf16[256,2048]{0,1:T(8,128)(2,1)} async-done(((bf16[2048,2048]{0,1:T(8,128)(2,1)}), bf16[256,2048]{0,1:T(8,128)(2,1)}) %reduce-scatter.13.cloned.1.call-update) | async-done | bytes 1048592 | tf_op jit(solution)/shard_map/reduce_scatter | solution.py:108
  578.4 27.6 %reduce-scatter.11.cloned.1.call-done = bf16[128,2048]{1,0:T(8,128)(2,1)} async-done(((bf16[512,2048]{1,0:T(8,128)(2,1)}), bf16[128,2048]{1,0:T(8,128)(2,1)}) %reduce-scatter.11.cloned.1.call-update) | async-done | bytes 524304 | tf_op jit(solution)/shard_map/reduce_scatter | solution.py:97
  620.6 8.4 all-gather.21.cloned.1.call-done
  650.5 51.2 %reduce-scatter.21.cloned.1.call-done = bf16[128,1024]{1,0:T(8,128)(2,1)} async-done(((bf16[1024,1024]{1,0:T(8,128)(2,1)}), bf16[128,1024]{1,0:T(8,128)(2,1)}) %reduce-scatter.21.cloned.1.call-update) | async-done | bytes 262160 | tf_op jit(solution)/shard_map/reduce_scatter | solution.py:108
  707.2 65.3 %reduce-scatter.23.cloned.1.call-done = bf16[128,1024]{1,0:T(8,128)(2,1)} async-done(((bf16[1024,1024]{1,0:T(8,128)(2,1)}), bf16[128,1024]{1,0:T(8,128)(2,1)}) %reduce-scatter.23.cloned.1.call-update) | async-done | bytes 262160 | tf_op jit(solution)/shard_map/reduce_scatter | solution.py:108
  777.9 5.9 fusion.32
  798.5 39.0 %reduce-scatter.19.cloned.1.call-done = bf16[32,1024]{1,0:T(8,128)(2,1)} async-done(((bf16[256,1024]{1,0:T(8,128)(2,1)}), bf16[32,1024]{1,0:T(8,128)(2,1)}) %reduce-scatter.19.cloned.1.call-update) | async-done | bytes 65552 | tf_op jit(solution)/shard_map/reduce_scatter | solution.py:108
  839.0 24.7 %reduce-scatter.15.cloned.1.call-done = bf16[128,1024]{1,0:T(8,128)(2,1)} async-done(((bf16[512,1024]{1,0:T(8,128)(2,1)}), bf16[128,1024]{1,0:T(8,128)(2,1)}) %reduce-scatter.15.cloned.1.call-update) | async-done | bytes 262160 | tf_op jit(solution)/shard_map/reduce_scatter | solution.py:97
  865.0 40.0 %all-reduce = (f32[8,1024]{1,0:T(8,128)S(1)}, f32[4]{0:T(128)S(1)}) all-reduce(f32[8,1024]{1,0:T(8,128)S(1)} %pad_maximum_fusion.8, f32[4]{0:T(128)S(1)} %pad_maximum_fusion.10), channel_id=1, replica_groups=mesh['dp'=8,'expert'=4] {'dp','expert'}, use_global_device_ids=true, to_apply=%region_26.27 | all-reduce | flops 8196 | bytes 65568 | tf_op jit(solution)/shard_map/psum | solution.py:303
  908.8 24.0 %reduce-scatter.17.cloned.1.call-done = bf16[128,768]{1,0:T(8,128)(2,1)} async-done(((bf16[1024,768]{1,0:T(8,128)(2,1)}), bf16[128,768]{1,0:T(8,128)(2,1)}) %reduce-scatter.17.cloned.1.call-update) | async-done | bytes 196624 | tf_op jit(solution)/shard_map/reduce_scatter | solution.py:108
  (226 shorter events, 141.9 us)
Async XLA Ops:
  7.2 291.1 %copy-start = (bf16[512,1,1024]{2,0,1:T(8,128)(2,1)S(1)}, bf16[512,1,1024]{2,0,1:T(8,128)(2,1)}, u32[]{:S(2)}) copy-start(bf16[512,1,1024]{2,0,1:T(8,128)(2,1)} %param.26) | copy-start | bytes 3145732
  7.2 106.8 %all-gather.9.cloned.1.call-start = ((), (), s32[]{:S(2)}) async-start(), calls=%async_computation.16 | async-start | bytes 1310720 | tf_op jit(solution)/shard_map/all_gather | solution.py:94
  55.8 60.6 %all-gather.11.cloned.1.call-start = ((), (), s32[]{:S(2)}) async-start(), calls=%async_computation.17 | async-start | bytes 1769472 | tf_op jit(solution)/shard_map/all_gather | solution.py:105
  101.7 12.3 %all-to-all-start.1 = ((bf16[4,64,1024]{2,1,0:T(8,128)(2,1)}), bf16[4,64,1024]{2,1,0:T(8,128)(2,1)S(1)}, u32[]{:S(2)}, u32[]{:S(2)}) async-start(bf16[4,64,1024]{2,1,0:T(8,128)(2,1)} %bitcast.11), calls=%async_computation.1 | async-start | bytes 1048576 | tf_op jit(solution)/shard_map/all_to_all | solution.py:102
  105.2 46.3 %reduce-scatter.9.cloned.1.call-start = ((), (), s32[]{:S(2)}) async-start(), calls=%async_computation.18 | async-start | bytes 1310720 | tf_op jit(solution)/shard_map/reduce_scatter | solution.py:97
  128.1 170.2 %all-gather.19.cloned.1.call-start = ((), (), s32[]{:S(2)}) async-start(), calls=%async_computation.23 | async-start | bytes 9437184 | tf_op jit(solution)/shard_map/all_gather | solution.py:105
  173.7 174.5 %all-gather.15.cloned.1.call-start = ((), (), s32[]{:S(2)}) async-start(), calls=%async_computation.20 | async-start | bytes 2359296 | tf_op jit(solution)/shard_map/all_gather | solution.py:105
  183.1 188.1 %all-gather.13.cloned.1.call-start = ((), (), s32[]{:S(2)}) async-start(), calls=%async_computation.19 | async-start | bytes 2621440 | tf_op jit(solution)/shard_map/all_gather | solution.py:94
  184.1 238.5 %all-gather.17.cloned.1.call-start = ((), (), s32[]{:S(2)}) async-start(), calls=%async_computation.21 | async-start | bytes 2359296 | tf_op jit(solution)/shard_map/all_gather | solution.py:105
  184.8 118.3 %copy-start.34 = (bf16[512,1,1024]{2,0,1:T(8,128)(2,1)S(1)}, bf16[512,1,1024]{2,0,1:T(8,128)(2,1)}, u32[]{:S(2)}) copy-start(bf16[512,1,1024]{2,0,1:T(8,128)(2,1)} %param.27) | copy-start | bytes 3145732
  184.8 387.7 %reduce-scatter.13.cloned.1.call-start = ((), (), s32[]{:S(2)}) async-start(), calls=%async_computation.24 | async-start | bytes 9437184 | tf_op jit(solution)/shard_map/reduce_scatter | solution.py:108
  325.2 280.8 %reduce-scatter.11.cloned.1.call-start = ((), (), s32[]{:S(2)}) async-start(), calls=%async_computation.22 | async-start | bytes 2621440 | tf_op jit(solution)/shard_map/reduce_scatter | solution.py:97
  574.8 32.3 %all-to-all-start.4 = ((bf16[4,64,2048]{2,1,0:T(8,128)(2,1)}), bf16[4,64,2048]{2,1,0:T(8,128)(2,1)S(1)}, u32[]{:S(2)}, u32[]{:S(2)}) async-start(bf16[4,64,2048]{2,1,0:T(8,128)(2,1)} %bitcast.27), calls=%async_computation.7 | async-start | bytes 2097152 | tf_op jit(solution)/shard_map/all_to_all | solution.py:102
  578.3 50.7 %all-gather.21.cloned.1.call-start = ((), (), s32[]{:S(2)}) async-start(), calls=%async_computation.25 | async-start | bytes 1310720 | tf_op jit(solution)/shard_map/all_gather | solution.py:94
  612.1 89.5 %reduce-scatter.21.cloned.1.call-start = ((), (), s32[]{:S(2)}) async-start(), calls=%async_computation.29 | async-start | bytes 2359296 | tf_op jit(solution)/shard_map/reduce_scatter | solution.py:108
  616.1 156.4 %reduce-scatter.23.cloned.1.call-start = ((), (), s32[]{:S(2)}) async-start(), calls=%async_computation.30 | async-start | bytes 2359296 | tf_op jit(solution)/shard_map/reduce_scatter | solution.py:108
  631.6 12.3 %all-to-all-start.6 = ((bf16[4,2,32,1024]{3,2,1,0:T(8,128)(2,1)}), bf16[4,2,32,1024]{3,2,1,0:T(8,128)(2,1)S(1)}, u32[]{:S(2)}, u32[]{:S(2)}) async-start(bf16[4,2,32,1024]{3,2,1,0:T(8,128)(2,1)} %bitcast.149), calls=%async_computation.11 | async-start | bytes 1048576 | tf_op jit(solution)/shard_map/all_to_all | solution.py:102
  635.1 202.4 %reduce-scatter.19.cloned.1.call-start = ((), (), s32[]{:S(2)}) async-start(), calls=%async_computation.28 | async-start | bytes 589824 | tf_op jit(solution)/shard_map/reduce_scatter | solution.py:108
  644.7 219.1 %reduce-scatter.15.cloned.1.call-start = ((), (), s32[]{:S(2)}) async-start(), calls=%async_computation.26 | async-start | bytes 1310720 | tf_op jit(solution)/shard_map/reduce_scatter | solution.py:97
  703.4 72.3 %copy-start.35 = (bf16[512,1024]{1,0:T(8,128)(2,1)S(1)}, bf16[512,1024]{1,0:T(8,128)(2,1)}, u32[]{:S(2)}) copy-start(bf16[512,1024]{1,0:T(8,128)(2,1)} %all-gather.9.cloned.1.call-done) | copy-start | bytes 3145732
  703.4 70.9 %all-to-all-start.7 = ((bf16[4,32,8,128]{3,2,1,0:T(8,128)(2,1)}), bf16[4,32,8,128]{3,2,1,0:T(8,128)(2,1)S(1)}, u32[]{:S(2)}, u32[]{:S(2)}) async-start(bf16[4,32,8,128]{3,2,1,0:T(8,128)(2,1)} %bitcast.74), calls=%async_computation.14 | async-start | bytes 524288 | tf_op jit(solution)/shard_map/all_to_all | solution.py:102
  706.9 225.9 %reduce-scatter.17.cloned.1.call-start = ((), (), s32[]{:S(2)}) async-start(), calls=%async_computation.27 | async-start | bytes 1769472 | tf_op jit(solution)/shard_map/reduce_scatter | solution.py:108
  791.9 114.8 %copy-start.11 = (f32[128,1024]{1,0:T(8,128)S(1)}, f32[128,1024]{1,0:T(8,128)}, u32[]{:S(2)}) copy-start(f32[128,1024]{1,0:T(8,128)} %get-tuple-element.112) | copy-start | bytes 1572868
  934.6 8.6 all-to-all-start.5
  (38 other events, 504.0 us)
Sparse Core Ops, SparseCore 0:
  55.9 14.9 all-gather.8
  73.6 42.6 all-gather.10
  128.2 23.1 reduce-scatter.8
  173.8 124.4 all-gather.18
  300.9 47.2 all-gather.14
  350.1 21.0 all-gather.12
  373.4 49.0 all-gather.16
  426.1 146.3 reduce-scatter.12
  575.7 30.2 reduce-scatter.10
  612.3 16.6 all-gather.20
  633.1 68.4 reduce-scatter.20
  705.0 67.3 reduce-scatter.22
  775.8 61.6 reduce-scatter.18
  839.9 23.7 reduce-scatter.14
  867.0 65.7 reduce-scatter.16
where the time goes:
time: 958 us; the launch traced here: 951 us
  waiting for transfers between devices  626 us (65%)
  blocking collectives  153 us (16%)
  matrix products  78 us (8%)
  other arithmetic  34 us (4%)
  local copies, waits for them, and re-layouts  25.2 us (3%)
  starting transfers between devices  18.8 us (2%)
  between operations  15.8 us (2%)
    reduce_scatter x5, waiting for transfers between devices, scatter_dp(): lax.psum_scatter(rows.astype(jnp.bfloat16), 'dp', scatter_dimension=0, ti...  319 us
    all_gather x4, waiting for transfers between devices, gather_dp(): return lax.all_gather(rows, 'dp', axis=0, tiled=True)  185 us
    reduce_scatter x3, waiting for transfers between devices, fold(): lax.psum_scatter(partial_sums.astype(jnp.bfloat16), 'expert', scatter_dim...  75.4 us
    all_gather x1, blocking collectives, per_device(): lax.all_gather(jnp.concatenate([norm1_gain[:, None], norm2_gain[:, None],...  43.4 us
    psum x1, blocking collectives, per_device(): lax.psum((jnp.concatenate([grad_gain_one[None], grad_gain_two[None], grad...  40 us
    all_to_all x3, blocking collectives, swap(): lax.all_to_all(blocks, 'expert', split_axis=0, concat_axis=0, tiled=True)  36.1 us
    all_gather x1, blocking collectives, gather_dp(): return lax.all_gather(rows, 'dp', axis=0, tiled=True)  33.8 us
    all_gather x3, waiting for transfers between devices, spread(): return lax.all_gather(rows_low, 'expert', axis=0, tiled=True)  31.6 us
  transfers between devices with their start and end apart: 20, of which 17 were waited for; matrix products, arithmetic and copies ran while one was open for 11% of the time, Pallas kernels for 0%

commit v1 on v0

--- a/solution.py
+++ b/solution.py
@@ -1,3 +1,4 @@
+import functools
 import jax
 import jax.numpy as jnp
 from jax import lax
@@ -9,6 +10,27 @@
 HIGHEST = lax.Precision.HIGHEST
 ROWS_AXIS = (((0,), (0,)), ((), ()))
 COLS_AXIS = (((1,), (1,)), ((), ()))
+
+
+def supply_signs_all(block_here, along_axis):
+    axis_total = jax.lax.axis_size(along_axis)
+    queue = [(dev_j, (dev_j + 1) % axis_total) for dev_j in range(axis_total)]
+    slots = [(dev_j, (dev_j - 1) % axis_total) for dev_j in range(axis_total)]
+    arr_out, current_arr = ([block_here], [block_here])
+    for _ in range(axis_total // 2):
+        s_next = jax.lax.ppermute(arr_out[-1], along_axis, queue)
+        arr_out.append(s_next)
+    ii = 0
+    while ii < (axis_total - 1) // 2:
+        view_out = jax.lax.ppermute(current_arr[-1], along_axis, slots)
+        current_arr.append(view_out)
+        ii = ii + 1
+    h_now = jnp.concatenate([*arr_out[::-1], *current_arr[1:]], 0)
+    arr_now = jax.lax.axis_index(along_axis)
+    return jnp.roll(h_now, (arr_now - axis_total // 2) * block_here.shape[0], 0)
+
+
+create_orders = functools.partial(supply_signs_all, along_axis="expert")
 
 
 def layer_norm(values, norm_gain):
@@ -91,7 +113,7 @@
     ff_own = replicas * ff_share
 
     def spread(rows_low):
-        return lax.all_gather(rows_low, "expert", axis=0, tiled=True)
+        return create_orders(rows_low)
 
     def fold(partial_sums):
         return lax.psum_scatter(

time: 958 us -> 915 us (0.955)
  waiting for transfers between devices: 626 us -> 559 us
    ppermute x0 -> x9, waiting for transfers between devices: none -> 34.5 us  [the longest x6 31.6 us: supply_signs_all(): s_next = jax.lax.ppermute(arr_out[-1], along_axis, queue)]
    all_gather x3 -> x0, waiting for transfers between devices: 31.6 us -> none  [spread(): return lax.all_gather(rows_low, 'expert', axis=0, tiled=True)]
    reduce_scatter x5, waiting for transfers between devices: 319 us -> 289 us  [scatter_dp(): lax.psum_scatter(rows.astype(jnp.bfloat16), 'dp', scatter_dimension=0, ti...]
    all_gather x4, waiting for transfers between devices: 185 us -> 155 us  [gather_dp(): return lax.all_gather(rows, 'dp', axis=0, tiled=True)]
  transfers between devices with their start and end apart: 20 -> 26, of which waited for: 17 -> 19; matrix products, arithmetic and copies ran while one was open for 11% -> 14% of each run, Pallas kernels for 0% -> 0%
where the time goes in v1:
time: 915 us; the launch traced here: 905 us
  waiting for transfers between devices  559 us (61%)
  blocking collectives  150 us (16%)
  matrix products  81.6 us (9%)
  other arithmetic  38.8 us (4%)
  local copies, waits for them, and re-layouts  34.4 us (4%)
  starting transfers between devices  25.2 us (3%)
  between operations  15.9 us (2%)
    reduce_scatter x5, waiting for transfers between devices, scatter_dp(): lax.psum_scatter(rows.astype(jnp.bfloat16), 'dp', scatter_dimension=0, ti...  289 us
    all_gather x4, waiting for transfers between devices, gather_dp(): return lax.all_gather(rows, 'dp', axis=0, tiled=True)  155 us
    reduce_scatter x3, waiting for transfers between devices, fold(): lax.psum_scatter(partial_sums.astype(jnp.bfloat16), 'expert', scatter_dim...  68.4 us
    all_gather x1, blocking collectives, per_device(): lax.all_gather(jnp.concatenate([norm1_gain[:, None], norm2_gain[:, None],...  41.4 us
    psum x1, blocking collectives, per_device(): lax.psum((jnp.concatenate([grad_gain_one[None], grad_gain_two[None], grad...  40 us
    all_to_all x3, blocking collectives, swap(): lax.all_to_all(blocks, 'expert', split_axis=0, concat_axis=0, tiled=True)  35.4 us
    all_gather x1, blocking collectives, gather_dp(): return lax.all_gather(rows, 'dp', axis=0, tiled=True)  33.2 us
    ppermute x6, waiting for transfers between devices, supply_signs_all(): s_next = jax.lax.ppermute(arr_out[-1], along_axis, queue)  31.6 us
  transfers between devices with their start and end apart: 26, of which 19 were waited for; matrix products, arithmetic and copies ran while one was open for 14% of the time, Pallas kernels for 0%

profile of v1, /device:TPU:0, one launch (start us, length us, event | category | flops | bytes accessed | tf_op | source)
XLA Modules:
  0.0 905.3 jit_solution(13346867357379011866)
XLA Ops:
  8.5 9.4 %all_to_all.40 = bf16[4,32,3,256]{3,1,2,0:T(8,128)(2,1)S(1)} all-to-all(bf16[4,32,3,256]{3,1,2,0:T(8,128)(2,1)S(1)} %copy.96), channel_id=1, replica_groups=mesh['dp'=8,'expert'=4] {'expert'}, dimensions={0} | all-to-all | bytes 393216 | tf_op jit(solution)/shard_map/all_to_all | solution.py:124
  18.8 41.4 %all-gather = bf16[32,32,8]{1,2,0:T(8,128)(2,1)S(1)} all-gather(bf16[1,32,8]{1,2,0:T(8,128)(2,1)S(1)} %maximum_bitcast_fusion), channel_id=1, replica_groups=mesh['dp'=8,'expert'=4] {'dp','expert'}, dimensions={0}, use_global_device_ids=true | all-gather | bytes 16896 | tf_op jit(solution)/shard_map/all_gather | solution.py:132
  61.4 33.2 %all_gather.20 = bf16[256,1024]{1,0:T(8,128)(2,1)} all-gather(bf16[32,1024]{1,0:T(8,128)(2,1)S(1)} %copy-done.22), channel_id=1, replica_groups=mesh['dp'=8,'expert'=4] {'dp'}, dimensions={0}, use_global_device_ids=true | all-gather | bytes 589824 | tf_op jit(solution)/shard_map/all_gather | solution.py:127
  101.4 6.0 all-to-all-done.1
  131.5 21.7 %reduce-scatter.9.cloned.1.call-done = bf16[128,1024]{1,0:T(8,128)(2,1)} async-done(((bf16[512,1024]{1,0:T(8,128)(2,1)}), bf16[128,1024]{1,0:T(8,128)(2,1)}) %reduce-scatter.9.cloned.1.call-update) | async-done | bytes 262160 | tf_op jit(solution)/shard_map/reduce_scatter | solution.py:119
  157.9 17.6 %all_to_all.41 = bf16[4,64,2048]{2,1,0:T(8,128)(2,1)} all-to-all(bf16[4,64,2048]{2,1,0:T(8,128)(2,1)S(1)} %bitcast.154), channel_id=1, replica_groups=mesh['dp'=8,'expert'=4] {'expert'}, dimensions={0} | all-to-all | bytes 2097152 | tf_op jit(solution)/shard_map/all_to_all | solution.py:124
  175.8 8.4 all_to_all.42
  185.7 114.4 %all-gather.12.cloned.1.call-done = bf16[2048,2048]{1,0:T(8,128)(2,1)} async-done(((bf16[256,2048]{1,0:T(8,128)(2,1)}), bf16[2048,2048]{1,0:T(8,128)(2,1)}) %all-gather.12.cloned.1.call-update) | async-done | bytes 8388624 | tf_op jit(solution)/shard_map/all_gather | solution.py:127
  318.6 8.4 pad_maximum_fusion
  327.2 8.6 collective-permute-done.3
  337.7 10.1 %collective-permute-done.4 = bf16[128,2048]{1,0:T(8,128)(2,1)S(1)} collective-permute-done((bf16[128,2048]{1,0:T(8,128)(2,1)S(1)}, bf16[128,2048]{1,0:T(8,128)(2,1)S(1)}, u32[]{:S(2)}, u32[]{:S(2)}) %collective-permute-start.4) | collective-permute-done | bytes 524320 | tf_op jit(solution)/shard_map/ppermute | solution.py:21
  359.1 40.5 %all-gather.10.cloned.1.call-done = bf16[1024,1024]{1,0:T(8,128)(2,1)} async-done(((bf16[128,1024]{1,0:T(8,128)(2,1)}), bf16[1024,1024]{1,0:T(8,128)(2,1)}) %all-gather.10.cloned.1.call-update) | async-done | bytes 2097168 | tf_op jit(solution)/shard_map/all_gather | solution.py:127
  399.6 5.0 fusion.25
  413.8 135.7 %reduce-scatter.13.cloned.1.call-done = bf16[256,2048]{0,1:T(8,128)(2,1)} async-done(((bf16[2048,2048]{0,1:T(8,128)(2,1)}), bf16[256,2048]{0,1:T(8,128)(2,1)}) %reduce-scatter.13.cloned.1.call-update) | async-done | bytes 1048592 | tf_op jit(solution)/shard_map/reduce_scatter | solution.py:130
  561.1 21.8 %reduce-scatter.11.cloned.1.call-done = bf16[128,2048]{1,0:T(8,128)(2,1)} async-done(((bf16[512,2048]{1,0:T(8,128)(2,1)}), bf16[128,2048]{1,0:T(8,128)(2,1)}) %reduce-scatter.11.cloned.1.call-update) | async-done | bytes 524304 | tf_op jit(solution)/shard_map/reduce_scatter | solution.py:119
  591.2 6.2 collective-permute-done.6
  597.8 5.8 collective-permute-done.7
  629.5 25.2 %reduce-scatter.21.cloned.1.call-done = bf16[128,1024]{1,0:T(8,128)(2,1)} async-done(((bf16[1024,1024]{1,0:T(8,128)(2,1)}), bf16[128,1024]{1,0:T(8,128)(2,1)}) %reduce-scatter.21.cloned.1.call-update) | async-done | bytes 262160 | tf_op jit(solution)/shard_map/reduce_scatter | solution.py:130
  660.2 65.5 %reduce-scatter.23.cloned.1.call-done = bf16[128,1024]{1,0:T(8,128)(2,1)} async-done(((bf16[1024,1024]{1,0:T(8,128)(2,1)}), bf16[128,1024]{1,0:T(8,128)(2,1)}) %reduce-scatter.23.cloned.1.call-update) | async-done | bytes 262160 | tf_op jit(solution)/shard_map/reduce_scatter | solution.py:130
  732.2 5.9 fusion.32
  752.8 38.5 %reduce-scatter.19.cloned.1.call-done = bf16[32,1024]{1,0:T(8,128)(2,1)} async-done(((bf16[256,1024]{1,0:T(8,128)(2,1)}), bf16[32,1024]{1,0:T(8,128)(2,1)}) %reduce-scatter.19.cloned.1.call-update) | async-done | bytes 65552 | tf_op jit(solution)/shard_map/reduce_scatter | solution.py:130
  792.8 24.9 %reduce-scatter.15.cloned.1.call-done = bf16[128,1024]{1,0:T(8,128)(2,1)} async-done(((bf16[512,1024]{1,0:T(8,128)(2,1)}), bf16[128,1024]{1,0:T(8,128)(2,1)}) %reduce-scatter.15.cloned.1.call-update) | async-done | bytes 262160 | tf_op jit(solution)/shard_map/reduce_scatter | solution.py:119
  818.9 40.0 %all-reduce = (f32[8,1024]{1,0:T(8,128)S(1)}, f32[4]{0:T(128)S(1)}) all-reduce(f32[8,1024]{1,0:T(8,128)S(1)} %pad_maximum_fusion.8, f32[4]{0:T(128)S(1)} %pad_maximum_fusion.10), channel_id=1, replica_groups=mesh['dp'=8,'expert'=4] {'dp','expert'}, use_global_device_ids=true, to_apply=%region_26.28 | all-reduce | flops 8196 | bytes 65568 | tf_op jit(solution)/shard_map/psum | solution.py:325
  862.7 23.9 %reduce-scatter.17.cloned.1.call-done = bf16[128,768]{1,0:T(8,128)(2,1)} async-done(((bf16[1024,768]{1,0:T(8,128)(2,1)}), bf16[128,768]{1,0:T(8,128)(2,1)}) %reduce-scatter.17.cloned.1.call-update) | async-done | bytes 196624 | tf_op jit(solution)/shard_map/reduce_scatter | solution.py:130
  (241 shorter events, 171.2 us)
Async XLA Ops:
  7.3 109.0 %all-gather.6.cloned.1.call-start = ((), (), s32[]{:S(2)}) async-start(), calls=%async_computation.16 | async-start | bytes 1769472 | tf_op jit(solution)/shard_map/all_gather | solution.py:127
  61.0 39.5 %collective-permute-start = (bf16[128,1024]{1,0:T(8,128)(2,1)S(1)}, bf16[128,1024]{1,0:T(8,128)(2,1)S(1)}, u32[]{:S(2)}, u32[]{:S(2)}) collective-permute-start(bf16[128,1024]{1,0:T(8,128)(2,1)S(1)} %fusion.74), channel_id=1, source_target_pairs={{0,1},{1,2},{2,3},{3,0},{4,5},{5,6},{6,7},{7,4},{8,9},{9,10},{10,1... | collective-permute-start | bytes 786440 | tf_op jit(solution)/shard_map/ppermute | solution.py:21
  94.6 12.8 %all-to-all-start.1 = ((bf16[4,64,1024]{2,1,0:T(8,128)(2,1)}), bf16[4,64,1024]{2,1,0:T(8,128)(2,1)S(1)}, u32[]{:S(2)}, u32[]{:S(2)}) async-start(bf16[4,64,1024]{2,1,0:T(8,128)(2,1)} %bitcast.11), calls=%async_computation.1 | async-start | bytes 1048576 | tf_op jit(solution)/shard_map/all_to_all | solution.py:124
  98.1 55.2 %reduce-scatter.9.cloned.1.call-start = ((), (), s32[]{:S(2)}) async-start(), calls=%async_computation.17 | async-start | bytes 1310720 | tf_op jit(solution)/shard_map/reduce_scatter | solution.py:119
  98.1 12.3 %collective-permute-start.2 = (bf16[128,1024]{1,0:T(8,128)(2,1)S(1)}, bf16[128,1024]{1,0:T(8,128)(2,1)S(1)}, u32[]{:S(2)}, u32[]{:S(2)}) collective-permute-start(bf16[128,1024]{1,0:T(8,128)(2,1)S(1)} %fusion.74), channel_id=1, source_target_pairs={{0,3},{1,0},{2,1},{3,2},{4,7},{5,4},{6,5},{7,6},{8,11},{9,8},{10,9... | collective-permute-start | bytes 786440 | tf_op jit(solution)/shard_map/ppermute | solution.py:25
  100.5 11.6 %collective-permute-start.1 = (bf16[128,1024]{1,0:T(8,128)(2,1)S(1)}, bf16[128,1024]{1,0:T(8,128)(2,1)}, u32[]{:S(2)}, u32[]{:S(2)}) collective-permute-start(bf16[128,1024]{1,0:T(8,128)(2,1)S(1)} %collective-permute-done), channel_id=1, source_target_pairs={{0,1},{1,2},{2,3},{3,0},{4,5},{5,6},{6,7},{7,4},{8,9},{9,10},{10,1... | collective-permute-start | bytes 786440 | tf_op jit(solution)/shard_map/ppermute | solution.py:21
  131.3 168.8 %all-gather.12.cloned.1.call-start = ((), (), s32[]{:S(2)}) async-start(), calls=%async_computation.21 | async-start | bytes 9437184 | tf_op jit(solution)/shard_map/all_gather | solution.py:127
  175.5 179.1 %all-gather.8.cloned.1.call-start = ((), (), s32[]{:S(2)}) async-start(), calls=%async_computation.18 | async-start | bytes 2359296 | tf_op jit(solution)/shard_map/all_gather | solution.py:127
  184.9 214.7 %all-gather.10.cloned.1.call-start = ((), (), s32[]{:S(2)}) async-start(), calls=%async_computation.19 | async-start | bytes 2359296 | tf_op jit(solution)/shard_map/all_gather | solution.py:127
  185.5 364.0 %reduce-scatter.13.cloned.1.call-start = ((), (), s32[]{:S(2)}) async-start(), calls=%async_computation.22 | async-start | bytes 9437184 | tf_op jit(solution)/shard_map/reduce_scatter | solution.py:130
  327.0 255.9 %reduce-scatter.11.cloned.1.call-start = ((), (), s32[]{:S(2)}) async-start(), calls=%async_computation.20 | async-start | bytes 2621440 | tf_op jit(solution)/shard_map/reduce_scatter | solution.py:119
  327.1 8.7 collective-permute-start.3
  335.8 12.0 %collective-permute-start.4 = (bf16[128,2048]{1,0:T(8,128)(2,1)S(1)}, bf16[128,2048]{1,0:T(8,128)(2,1)S(1)}, u32[]{:S(2)}, u32[]{:S(2)}) collective-permute-start(bf16[128,2048]{1,0:T(8,128)(2,1)S(1)} %collective-permute-done.3), channel_id=1, source_target_pairs={{0,1},{1,2},{2,3},{3,0},{4,5},{5,6},{6,7},{7,4},{8,9},{9,10},{10,1... | collective-permute-start | bytes 1572872 | tf_op jit(solution)/shard_map/ppermute | solution.py:21
  335.8 14.6 %collective-permute-start.5 = (bf16[128,2048]{1,0:T(8,128)(2,1)}, bf16[128,2048]{1,0:T(8,128)(2,1)S(1)}, u32[]{:S(2)}, u32[]{:S(2)}) collective-permute-start(bf16[128,2048]{1,0:T(8,128)(2,1)} %copy-done.16), channel_id=1, source_target_pairs={{0,3},{1,0},{2,1},{3,2},{4,7},{5,4},{6,5},{7,6},{8,11},{9,8},{10,9... | collective-permute-start | bytes 1572872 | tf_op jit(solution)/shard_map/ppermute | solution.py:25
  409.8 244.9 %reduce-scatter.21.cloned.1.call-start = ((), (), s32[]{:S(2)}) async-start(), calls=%async_computation.26 | async-start | bytes 2359296 | tf_op jit(solution)/shard_map/reduce_scatter | solution.py:130
  551.7 32.3 %all-to-all-start.4 = ((bf16[4,64,2048]{2,1,0:T(8,128)(2,1)}), bf16[4,64,2048]{2,1,0:T(8,128)(2,1)}, u32[]{:S(2)}, u32[]{:S(2)}) async-start(bf16[4,64,2048]{2,1,0:T(8,128)(2,1)} %bitcast.27), calls=%async_computation.7 | async-start | bytes 2097152 | tf_op jit(solution)/shard_map/all_to_all | solution.py:124
  556.0 169.7 %reduce-scatter.23.cloned.1.call-start = ((), (), s32[]{:S(2)}) async-start(), calls=%async_computation.27 | async-start | bytes 2359296 | tf_op jit(solution)/shard_map/reduce_scatter | solution.py:130
  589.5 8.4 collective-permute-start.8
  609.1 12.3 %all-to-all-start.6 = ((bf16[4,2,32,1024]{3,2,1,0:T(8,128)(2,1)}), bf16[4,2,32,1024]{3,2,1,0:T(8,128)(2,1)S(1)}, u32[]{:S(2)}, u32[]{:S(2)}) async-start(bf16[4,2,32,1024]{3,2,1,0:T(8,128)(2,1)} %bitcast.160), calls=%async_computation.11 | async-start | bytes 1048576 | tf_op jit(solution)/shard_map/all_to_all | solution.py:124
  612.6 178.7 %reduce-scatter.19.cloned.1.call-start = ((), (), s32[]{:S(2)}) async-start(), calls=%async_computation.25 | async-start | bytes 589824 | tf_op jit(solution)/shard_map/reduce_scatter | solution.py:130
  622.2 195.5 %reduce-scatter.15.cloned.1.call-start = ((), (), s32[]{:S(2)}) async-start(), calls=%async_computation.23 | async-start | bytes 1310720 | tf_op jit(solution)/shard_map/reduce_scatter | solution.py:119
  656.4 71.1 %all-to-all-start.7 = ((bf16[4,32,8,128]{3,2,1,0:T(8,128)(2,1)}), bf16[4,32,8,128]{3,2,1,0:T(8,128)(2,1)S(1)}, u32[]{:S(2)}, u32[]{:S(2)}) async-start(bf16[4,32,8,128]{3,2,1,0:T(8,128)(2,1)} %bitcast.74), calls=%async_computation.14 | async-start | bytes 524288 | tf_op jit(solution)/shard_map/all_to_all | solution.py:124
  660.0 226.7 %reduce-scatter.17.cloned.1.call-start = ((), (), s32[]{:S(2)}) async-start(), calls=%async_computation.24 | async-start | bytes 1769472 | tf_op jit(solution)/shard_map/reduce_scatter | solution.py:130
  888.4 8.6 all-to-all-start.5
  (42 other events, 781.0 us)
Sparse Core Ops, SparseCore 0:
  18.9 44.5 all-gather.5
  131.4 21.8 reduce-scatter.8
  175.6 124.4 all-gather.11
  302.7 47.2 all-gather.7
  351.9 47.6 all-gather.9
  403.1 146.3 reduce-scatter.12
  552.6 30.2 reduce-scatter.10
  586.4 68.2 reduce-scatter.20
  658.3 67.4 reduce-scatter.22
  729.5 61.7 reduce-scatter.18
  793.8 23.7 reduce-scatter.14
  820.9 65.7 reduce-scatter.16
